TPU v7x, 128 devices: a whole 4x4x4 slice. The times are simulated.
128 devices in a mesh: chord: 8 (over y_lo, z), span: 16 (over x, y_hi, core).
Axes of the slice: x: 4, y: 4 (y_hi: 2, y_lo: 2; y = y_hi * 2 + y_lo), z: 4, core: 2. Of those that a mesh axis runs over, the one named last changes fastest.
Arguments:
- state: float32 [5, 125, 32, 32, 128], P(None, None, 'chord', 'span'), may hold values from -10 to 10
Outputs:
- residual: float32 [5, 125, 32, 32, 128], P(None, None, 'chord', 'span')
- viscosity: float32 [125, 32, 32, 128], P(None, 'chord', 'span')
All inputs are finite; a program needn't handle non-finite values.
Results may differ from a plain program's by a relative error of at most 0.0001.
Values sent between devices are 32-bit elements; how exact they have to be, the bound alone decides.
No kernel may reach another device: no remote copies, remote signals or barrier semaphores. Data moves between devices by JAX's collectives and lax.ppermute only.
A program may use at most 128 MiB of HBM per device.

v0:
```python
import math

import jax
import jax.numpy as jnp
import numpy as np
from jax import lax
from jax.experimental import pallas as pl
from jax.experimental.pallas import tpu as pltpu
from jax.sharding import PartitionSpec as P


EPS_SCALE = 0.01
SENSOR_CENTRE = -3.0
SENSOR_WIDTH = 1.5
RATIO_FLOOR = 1e-06
ENERGY_EPS = 1e-06
GAUSS_NODES = [-0.906179845938664, -0.5384693101056831, 0.0, 0.5384693101056831, 0.906179845938664]
GAUSS_WEIGHTS = [
    0.2369268850561891,
    0.4786286704993665,
    0.5688888888888889,
    0.4786286704993665,
    0.2369268850561891,
]


def legendre_values(points):
    values = [np.ones(points.shape), np.array(points)]
    for order in range(1, 5):
        values.append(
            ((2 * order + 1) * points * values[order] - order * values[order - 1]) / (order + 1)
        )
    return values


def line_tables():
    line_nodes = np.array(GAUSS_NODES)
    quadrature_weights = np.array(GAUSS_WEIGHTS)
    barycentric = np.array(
        [
            1.0 / np.prod([line_nodes[j] - line_nodes[k] for k in range(5) if k != j])
            for j in range(5)
        ]
    )
    derivative = np.zeros((5, 5))
    for i in range(5):
        for j in range(5):
            if i != j:
                derivative[i, j] = barycentric[j] / barycentric[i] / (line_nodes[i] - line_nodes[j])
        derivative[i, i] = -np.sum(derivative[i])
    left_values = np.ones(5)
    right_values = np.ones(5)
    for j in range(5):
        for k in range(5):
            if k != j:
                left_values[j] *= (-1.0 - line_nodes[k]) / (line_nodes[j] - line_nodes[k])
                right_values[j] *= (1.0 - line_nodes[k]) / (line_nodes[j] - line_nodes[k])
    legendre = legendre_values(line_nodes)
    fourth_slope = 7.0 * legendre[3] + 3.0 * legendre[1]
    fifth_slope = 9.0 * legendre[4] + 5.0 * legendre[2] + legendre[0]
    modal = np.zeros((5, 5))
    for k in range(5):
        modal[k, :] = quadrature_weights * math.sqrt((2 * k + 1) / 2.0) * legendre[k]
    return (line_nodes, derivative, left_values, right_values, fourth_slope, fifth_slope, modal)


NODES, DERIV, LEFT, RIGHT, SLOPE4, SLOPE5, MODAL = line_tables()
CORR_L = 0.5 * (SLOPE4 - SLOPE5)
CORR_R = 0.5 * (SLOPE4 + SLOPE5)
OWN = DERIV - 0.5 * (np.outer(CORR_L, LEFT) + np.outer(CORR_R, RIGHT))
ROWS, LANES = 8, 128
NV, NF = 5, 25
SPAN_V, CHORD_V = 13, 7
SPAN_N, CHORD_N = NV * SPAN_V, NV * CHORD_V


def mul(scale, x):
    return float(scale) * x


def even_odd(x):
    return (x[0] + x[4], x[1] + x[3], x[0] - x[4], x[1] - x[3], x[2])


def traces(parts):
    e0, e1, o0, o1, c = parts
    even = (
        mul(0.5 * (LEFT[0] + LEFT[4]), e0) + mul(0.5 * (LEFT[1] + LEFT[3]), e1) + mul(LEFT[2], c)
    )
    odd = mul(0.5 * (LEFT[0] - LEFT[4]), o0) + mul(0.5 * (LEFT[1] - LEFT[3]), o1)
    return (even + odd, even - odd)


def slope(parts, total, diff):
    e0, e1, o0, o1, c = parts
    even, odd = [], []
    for i in range(3):
        even.append(
            mul(0.5 * (OWN[i, 0] - OWN[i, 4]), o0)
            + mul(0.5 * (OWN[i, 1] - OWN[i, 3]), o1)
            + mul(0.25 * SLOPE5[i], diff)
        )
    for i in range(2):
        odd.append(
            mul(0.5 * (OWN[i, 0] + OWN[i, 4]), e0)
            + mul(0.5 * (OWN[i, 1] + OWN[i, 3]), e1)
            + (mul(OWN[i, 2], c) + mul(0.25 * SLOPE4[i], total))
        )
    return [
        even[0] + odd[0],
        even[1] + odd[1],
        even[2],
        even[1] - odd[1],
        even[0] - odd[0],
    ]


def modal_line(x):
    e0, e1, o0, o1, c = even_odd(x)
    out = []
    for k in range(5):
        if k % 2 == 0:
            out.append(mul(MODAL[k, 0], e0) + mul(MODAL[k, 1], e1) + mul(MODAL[k, 2], c))
        else:
            out.append(mul(MODAL[k, 0], o0) + mul(MODAL[k, 1], o1))
    return out


def line_points(axis, f):
    a, b = f // 5, f % 5
    if axis == 0:
        return [25 * k + 5 * a + b for k in range(5)]
    if axis == 1:
        return [25 * a + 5 * k + b for k in range(5)]
    return [25 * a + 5 * b + k for k in range(5)]


def row_ids():
    rows = lax.broadcasted_iota(jnp.int32, (ROWS, LANES), 0)
    return (rows // 2, rows % 2)


def lane_ids():
    return lax.broadcasted_iota(jnp.int32, (ROWS, LANES), 1)


def up_rows(x, n):
    n = n % ROWS
    return x if n == 0 else pltpu.roll(x, n, 0)


def splat_flag(flag):
    return jnp.full((ROWS, LANES), flag.astype(jnp.int32), jnp.int32) > 0


def chord_ends():
    at = lax.axis_index("chord")
    return (splat_flag(at == 0), splat_flag(at == lax.axis_size("chord") - 1))


def even_span():
    return splat_flag(lax.axis_index("span") % 2 == 0)


def even_chord():
    return splat_flag(lax.axis_index("chord") % 2 == 0)


def pack_span(out_of, is_low, even, first_ref, second_ref, base, count=NF):
    for m in range((count + 1) // 2):
        f0 = out_of(2 * m)
        f1 = out_of(2 * m + 1) if 2 * m + 1 < count else f0
        up = jnp.where(is_low, up_rows(f0, -1), f1)
        down = jnp.where(is_low, f0, up_rows(f1, 1))
        first_ref[base + m] = jnp.where(even, up, down)
        second_ref[base + m] = jnp.where(even, down, up)


def pack_chord(out_of, i, even, first_ref, second_ref, base, count=NF):
    for m in range((count + 3) // 4):
        up = down = None
        for q in range(4):
            f = 4 * m + q
            if f >= count:
                continue
            trace = out_of(f)
            u, d = up_rows(trace, 2 * q - 6), up_rows(trace, 2 * q)
            up = u if up is None else jnp.where(i == q, u, up)
            down = d if down is None else jnp.where(i == q, d, down)
        first_ref[base + m] = jnp.where(even, up, down)
        second_ref[base + m] = jnp.where(even, down, up)


def open_span(below, above, q, is_low):
    if q == 0:
        return jnp.where(is_low, below, up_rows(above, 1))
    return jnp.where(is_low, up_rows(below, -1), above)


def open_chord(below, above, q, i):
    return jnp.where(i == 0, up_rows(below, -2 * q), up_rows(above, 6 - 2 * q))


def sided(even, first, second):
    return (jnp.where(even, second, first), jnp.where(even, first, second))


def sensor_kernel(source, eps, density, work, sem):
    read = pltpu.make_async_copy(source.at[0], density, sem)
    read.start()
    read.wait()
    eps[...] = sensor(density, work)


def leave_chord_kernel(state, co, ce):
    i, _ = row_ids()
    first_row = i == 0
    ec = even_chord()

    def one(v, carry):
        def leaving(f):
            left, right = traces(even_odd([state[v, p] for p in line_points(0, f)]))
            return jnp.where(first_row, left, right)

        pack_chord(leaving, i, ec, ce, co, v * CHORD_V)
        return carry

    lax.fori_loop(0, NV, one, 0)


def three_kernel(eps, rkce, rkco, traces_even, three, se):
    first, last = chord_ends()
    behind, ahead = sided(even_chord(), rkce[...], rkco[...])
    three[0] = eps[...]
    three[1] = jnp.where(first, 0.0, behind)
    three[2] = jnp.where(last, 0.0, ahead)
    for n in range(3):
        se[SPAN_N + n] = three[n]
    for m in range(SPAN_N):
        se[m] = traces_even[m]


def leave_span_kernel(state, so, se):
    _, j = row_ids()
    is_low = j == 0
    es = even_span()

    def one(v, carry):
        def leaving(f):
            left, right = traces(even_odd([state[v, p] for p in line_points(1, f)]))
            return jnp.where(is_low, left, right)

        pack_span(leaving, is_low, es, se, so, v * SPAN_V)
        return carry

    lax.fori_loop(0, NV, one, 0)


def sensor(density, work):
    for axis in range(2):
        origin = density if axis == 0 else work
        for f in range(NF):
            points = line_points(axis, f)
            for p, value in zip(points, modal_line([origin[p] for p in points])):
                work[p] = value
    low_sums, high_sums = [], []
    for f in range(NF):
        a, b = f // 5, f % 5
        low, high = None, None
        for k, value in enumerate(modal_line([work[p] for p in line_points(2, f)])):
            square = value * value
            if a == 4 or b == 4 or k == 4:
                high = square if high is None else high + square
            else:
                low = square if low is None else low + square
        if low is not None:
            low_sums.append(low)
        high_sums.append(high)

    def tree(values):
        while len(values) > 1:
            values = [
                values[n] + values[n + 1] if n + 1 < len(values) else values[n]
                for n in range(0, len(values), 2)
            ]
        return values[0]

    high_part = tree(high_sums)
    total = (tree(low_sums) + high_part) + ENERGY_EPS
    level = jnp.log(jnp.maximum(high_part / total, RATIO_FLOOR)) * (1.0 / math.log(10.0))
    ramp = jnp.clip((level - SENSOR_CENTRE) / SENSOR_WIDTH, -1.0, 1.0)
    eps = EPS_SCALE * 0.5 * (1.0 + jnp.sin(0.5 * math.pi * ramp))
    return eps


def neighbours_chord(left, right, sign, i):
    first = (lax.axis_index("chord") == 0).astype(jnp.float32) * sign
    last = (lax.axis_index("chord") == lax.axis_size("chord") - 1).astype(jnp.float32) * sign
    before = jnp.where(i == 0, left * first, up_rows(right, 2))
    after = jnp.where(i == 3, right * last, up_rows(left, -2))
    return (before + after, after - before)


def neighbours_span(left, right, is_low, sign_row):
    inner = jnp.where(is_low, up_rows(left, -1), up_rows(right, 1))
    return (inner, inner * sign_row)


def neighbours_normal(left, right, sign, lane):
    before = jnp.where(lane == 0, mul(sign, left), pltpu.roll(right, 1, 1))
    after = jnp.where(lane == LANES - 1, mul(sign, right), pltpu.roll(left, LANES - 1, 1))
    return (before + after, after - before)


def gradient_kernel(state, gc, gs):
    i, j = row_ids()
    is_low = j == 0
    sign_row = jnp.where(is_low, 1.0, -1.0)

    def one(v, carry):
        for axis, ref in ((0, gc), (1, gs)):
            for f in range(NF):
                points = line_points(axis, f)
                parts = even_odd([state[v, p] for p in points])
                left, right = traces(parts)
                if axis == 0:
                    total, diff = neighbours_chord(left, right, 1.0, i)
                else:
                    total, diff = neighbours_span(left, right, is_low, sign_row)
                for p, value in zip(points, slope(parts, total, diff)):
                    ref[v, p] = value
        return carry

    lax.fori_loop(0, NV, one, 0)


def viscosity_into(visc, own, behind, ahead):
    i, j = row_ids()
    lane = lane_ids()
    is_low = j == 0

    def chord_pair(mid, low, high):
        under = up_rows(jnp.where(i == 3, low, mid), 2)
        over = up_rows(jnp.where(i == 0, high, mid), -2)
        return (jnp.maximum(mid, under), jnp.maximum(mid, over))

    mids, befores, afters = (chord_pair(own[n], behind[n], ahead[n]) for n in range(3))
    corners = {}
    for x in range(2):
        mid, low, high = mids[x], befores[x], afters[x]
        under = jnp.where(is_low, up_rows(low, -1), up_rows(mid, 1))
        over = jnp.where(is_low, up_rows(mid, -1), up_rows(high, 1))
        for y, value in enumerate((jnp.maximum(mid, under), jnp.maximum(mid, over))):
            low_z = jnp.where(lane == 0, value, pltpu.roll(value, 1, 1))
            high_z = jnp.where(lane == LANES - 1, value, pltpu.roll(value, LANES - 1, 1))
            corners[x, y, 0] = jnp.maximum(value, low_z)
            corners[x, y, 1] = jnp.maximum(value, high_z)
    halves = [((1.0 - x) / 2.0, (1.0 + x) / 2.0) for x in NODES]
    for a in range(5):
        plane = {
            (y, z): mul(halves[a][0], corners[0, y, z]) + mul(halves[a][1], corners[1, y, z])
            for y in range(2)
            for z in range(2)
        }
        for b in range(5):
            low, high = (
                mul(halves[b][0], plane[0, z]) + mul(halves[b][1], plane[1, z]) for z in range(2)
            )
            for c in range(5):
                visc[25 * a + 5 * b + c] = mul(halves[c][0], low) + mul(halves[c][1], high)
    return corners


SHARE = 0.5 * LEFT * CORR_L
SHARE_FAR = float(np.sum(SHARE * (1.0 + NODES) / 2.0))
SHARE_NEAR = float(np.sum(SHARE * (1.0 - NODES) / 2.0))


def chord_send_kernel(gc, three, rkso, rse, visc, bco, bce, near):
    i, _ = row_ids()
    first_row = i == 0
    es, ec = even_span(), even_chord()
    corners = viscosity_into(
        visc, *((three[n],) + sided(es, rse[SPAN_N + n], rkso[n]) for n in range(3))
    )
    for n in range(4):
        y, z = n // 2, n % 2
        near[n] = SHARE_NEAR * jnp.where(first_row, -corners[0, y, z], corners[1, y, z])

    def far(n):
        return jnp.where(first_row, corners[1, n // 2, n % 2], corners[0, n // 2, n % 2])

    pack_chord(far, i, ec, bce, bco, CHORD_N, 4)

    def one(v, carry):
        def leaving(f):
            left, right = traces(even_odd([visc[p] * gc[v, p] for p in line_points(0, f)]))
            return jnp.where(first_row, left, right)

        pack_chord(leaving, i, ec, bce, bco, v * CHORD_V)
        return carry

    lax.fori_loop(0, NV, one, 0)


def span_flux_kernel(gs, visc, rse, rso, fs, bso, bse):
    _, j = row_ids()
    is_low = j == 0
    es = even_span()
    weights = span_weights(is_low)

    def one(v, carry):
        received = {}

        def leaving(f):
            m, q = f // 2, f % 2
            if m not in received:
                base = v * SPAN_V + m
                received[m] = sided(es, rse[base], rso[base])
            edge = open_span(received[m][0], received[m][1], q, is_low)
            values = []
            for k, p in enumerate(line_points(1, f)):
                value = visc[p] * (gs[v, p] + weights[k] * edge)
                fs[v, p] = value
                values.append(value)
            left, right = traces(even_odd(values))
            return jnp.where(is_low, left, right)

        pack_span(leaving, is_low, es, bse, bso, v * SPAN_V)
        return carry

    lax.fori_loop(0, NV, one, 0)


def factors_into(factor, far, near, behind_row):
    value = [
        jnp.where(behind_row, -SHARE_FAR, SHARE_FAR) * far[n] + near[n] for n in range(4)
    ]
    halves = [((1.0 - x) / 2.0, (1.0 + x) / 2.0) for x in NODES]
    for a in range(5):
        low, high = (
            mul(halves[a][0], value[z]) + mul(halves[a][1], value[2 + z]) for z in range(2)
        )
        for c in range(5):
            factor[5 * a + c] = mul(halves[c][0], low) + mul(halves[c][1], high)


def inner_kernel(state, visc, fs, gc, rce, rco, res, visc_out, total_ref, diff_ref, flux, sem):
    write = pltpu.make_async_copy(visc, visc_out, sem)
    write.start()
    i, j = row_ids()
    lane = lane_ids()
    is_low = j == 0
    sign_row = jnp.where(is_low, 1.0, -1.0)
    ec = even_chord()
    weights = chord_weights(i)

    def one(v, carry):
        received = {}

        def across(c):
            plane = {}
            for b in range(5):
                f = 5 * b + c
                m, q = f // 4, f % 4
                if m not in received:
                    at = v * CHORD_V + m
                    received[m] = sided(ec, rce[at], rco[at])
                edge = open_chord(*received[m], q, i)
                points = line_points(0, f)
                parts = even_odd(
                    [visc[p] * (gc[v, p] + weights[k] * edge) for k, p in enumerate(points)]
                )
                total, diff = neighbours_chord(*traces(parts), -1.0, i)
                plane.update(zip(points, slope(parts, total, diff)))
            for a in range(5):
                points = line_points(1, 5 * a + c)
                parts = even_odd([fs[v, p] for p in points])
                total, diff = neighbours_span(*traces(parts), is_low, sign_row)
                for p, value in zip(points, slope(parts, total, diff)):
                    res[v, p] = plane[p] + value

        for f in range(NF):
            ends = traces(even_odd([state[v, p] for p in line_points(2, f)]))
            total_ref[f], diff_ref[f] = neighbours_normal(*ends, 1.0, lane)
        across(0)
        across(1)
        for f in range(NF):
            points = line_points(2, f)
            parts = even_odd([state[v, p] for p in points])
            values = slope(parts, total_ref[f], diff_ref[f])
            values = [visc[p] * value for p, value in zip(points, values)]
            for p, value in zip(points, values):
                flux[p] = value
            ends = traces(even_odd(values))
            total_ref[NF + f], diff_ref[NF + f] = neighbours_normal(*ends, -1.0, lane)
        across(2)
        across(3)
        across(4)
        for f in range(NF):
            points = line_points(2, f)
            parts = even_odd([flux[p] for p in points])
            values = slope(parts, total_ref[NF + f], diff_ref[NF + f])
            for p, value in zip(points, values):
                res[v, p] = res[v, p] + value
        return carry

    lax.fori_loop(0, NV, one, 0)
    write.wait()


def close_chord_kernel(res, ce, co, rbce, rbco, near, out, factor):
    i, _ = row_ids()
    ec = even_chord()
    weights = chord_weights(i)
    far = sided(ec, rbce[CHORD_N], rbco[CHORD_N])
    factors_into(factor, [open_chord(*far, n, i) for n in range(4)], near, i == 0)

    def one(v, carry):
        for m in range(CHORD_V):
            at = v * CHORD_V + m
            received, own = sided(ec, rbce[at], rbco[at]), sided(ec, ce[at], co[at])
            for f in range(4 * m, min(4 * m + 4, NF)):
                q = f % 4
                edge = open_chord(*received, q, i) + factor[f] * open_chord(*own, q, i)
                for k, p in enumerate(line_points(0, f)):
                    out[v, p] = res[v, p] + weights[k] * edge
        return carry

    lax.fori_loop(0, NV, one, 0)


def close_span_kernel(res, rbse, rbso, final, out, sems):
    _, j = row_ids()
    is_low = j == 0
    es = even_span()
    weights = span_weights(is_low)

    def send(v, a):
        points = pl.ds(NF * a, NF)
        return pltpu.make_async_copy(out.at[v, points], final.at[v, points], sems.at[v, a])

    def one(v, carry):
        for m in range(SPAN_V):
            first, second = rbse[v * SPAN_V + m], rbso[v * SPAN_V + m]
            behind, ahead = jnp.where(es, second, first), jnp.where(es, first, second)
            for f in range(2 * m, min(2 * m + 2, NF)):
                edge = open_span(behind, ahead, f % 2, is_low)
                for k, p in enumerate(line_points(1, f)):
                    out[v, p] = res[v, p] + weights[k] * edge
                a, c = f // 5, f % 5
                if c == 4 and a > 0:
                    send(v, a - 1).start()
                elif c == 4:

                    @pl.when(v > 0)
                    def _():
                        send(v - 1, 4).start()

        return carry

    lax.fori_loop(0, NV, one, 0)
    send(NV - 1, 4).start()
    for v in range(NV):
        for a in range(5):
            send(v, a).wait()


def span_weights(is_low):
    return [jnp.where(is_low, float(0.5 * CORR_L[k]), float(0.5 * CORR_R[k])) for k in range(5)]


def chord_weights(i):
    first, last = chord_ends()
    low, high = jnp.logical_and(i == 0, ~first), jnp.logical_and(i == 3, ~last)
    return [
        jnp.where(low, float(0.5 * CORR_L[k]), jnp.where(high, float(0.5 * CORR_R[k]), 0.0))
        for k in range(5)
    ]


def held(*lead):
    return pltpu.VMEM(lead + (ROWS, LANES), jnp.float32)


def vec(*lead):
    return jax.ShapeDtypeStruct(lead + (ROWS, LANES), jnp.float32)


def call(kernel, outs, args, scratch=(), cycles=1000, far_in=(), far_out=(), grant=24 * 2**20):
    vmem, hbm = (pl.BlockSpec(memory_space=m) for m in (pltpu.VMEM, pltpu.HBM))
    total = sum(int(np.prod(x.shape)) for x in list(outs) + list(args)) * 4
    return pl.pallas_call(
        kernel,
        out_shape=outs,
        in_specs=[hbm if n in far_in else vmem for n in range(len(args))],
        out_specs=[hbm if n in far_out else vmem for n in range(len(outs))],
        scratch_shapes=list(scratch),
        compiler_params=pltpu.CompilerParams(vmem_limit_bytes=grant),
        cost_estimate=pl.CostEstimate(flops=cycles * 4096, bytes_accessed=total, transcendentals=0),
    )(*args)


def paired(n, odd, wraps):
    route = []
    for lower in range(odd, n, 2):
        upper = lower + 1
        if upper >= n:
            if not wraps:
                continue
            upper %= n
        route += [(lower, upper), (upper, lower)]
    return route


def shards(state):
    chords, spans = lax.axis_size("chord"), lax.axis_size("span")

    def span_swap(array, odd):
        return lax.ppermute(array, "span", paired(spans, odd, True))

    def chord_swap(array, odd):
        route = [
            (a * spans + c, b * spans + c) for a, b in paired(chords, odd, False) for c in range(spans)
        ]
        if odd:
            route += [
                (a * spans + c, a * spans + (c ^ 1)) for a in (0, chords - 1) for c in range(spans)
            ]
        return lax.ppermute(array, ("chord", "span"), route)

    dma = pltpu.SemaphoreType.DMA
    u = state.reshape(NV, 125, ROWS, LANES)
    (eps,) = call(
        sensor_kernel,
        [vec()],
        [pltpu.with_memory_space_constraint(u, pltpu.HBM)],
        [held(125), held(125), dma(())],
        far_in=(0,),
    )
    rkco = chord_swap(eps, 1)
    rkce = chord_swap(eps, 0)
    so, se = call(leave_span_kernel, [vec(SPAN_N), vec(SPAN_N)], [u])
    rso = span_swap(so, 1)
    three, se = call(three_kernel, [vec(3), vec(SPAN_N + 3)], [eps, rkce, rkco, se], cycles=100)
    rkso = span_swap(three, 1)
    co, ce = call(leave_chord_kernel, [vec(CHORD_N), vec(CHORD_N)], [u])
    rco = chord_swap(co, 1)
    rce = chord_swap(ce, 0)
    rse = span_swap(se, 0)
    gc, gs = call(gradient_kernel, [vec(NV, 125)] * 2, [u], cycles=4000)
    visc, bco, bce, near = call(
        chord_send_kernel,
        [vec(125), vec(CHORD_N + 1), vec(CHORD_N + 1), vec(4)],
        [gc, three, rkso, rse],
        cycles=2000,
    )
    rbco = chord_swap(bco, 1)
    fs, bso, bse = call(
        span_flux_kernel,
        [vec(NV, 125), vec(SPAN_N), vec(SPAN_N)],
        [gs, visc, rse, rso],
        cycles=2000,
    )
    rbso = span_swap(bso, 1)
    rbce = chord_swap(bce, 0)
    rbse = span_swap(bse, 0)
    res, visc_out = call(
        inner_kernel,
        [vec(NV, 125), vec(125)],
        [u, visc, fs, gc, rce, rco],
        [held(2 * NF), held(2 * NF), held(125), dma(())],
        cycles=8000,
        far_out=(1,),
    )
    (res,) = call(
        close_chord_kernel, [vec(NV, 125)], [res, ce, co, rbce, rbco, near], [held(NF)], cycles=1000
    )
    (out,) = call(
        close_span_kernel,
        [vec(NV, 125)],
        [res, rbse, rbso],
        [held(NV, 125), dma((NV, 5))],
        cycles=2000,
        far_out=(0,),
    )
    return (out.reshape(state.shape), visc_out.reshape(state.shape[1:]))


def solution(mesh):
    in_specs = (P(None, None, "chord", "span", None),)
    out_specs = (P(None, None, "chord", "span", None), P(None, "chord", "span", None))

    return jax.shard_map(shards, mesh=mesh, in_specs=in_specs, out_specs=out_specs, check_vma=False)
```

profile of v0, /device:TPU:15, one launch (start us, length us, event | category | flops | bytes accessed | tf_op | source)
XLA Modules:
  0.0 47.1 jit_solution(11759556021983878472)
XLA Ops:
  0.6 0.0 copy-start
  0.6 1.6 %shard_map.31.eps = f32[8,128]{1,0:T(8,128)S(1)} custom-call(f32[5,125,8,128]{3,2,1,0:T(8,128)} %bitcast.3), custom_call_target="tpu_custom_call" | custom-call | flops 4096000 | bytes 2564096 | tf_op jit(solution)/shard_map/pallas_call | solution.py:593
  2.2 1.7 %collective-permute-start = (f32[8,128]{1,0:T(8,128)S(1)}, f32[8,128]{1,0:T(8,128)S(1)}, u32[]{:S(2)}, u32[]{:S(2)}) collective-permute-start(f32[8,128]{1,0:T(8,128)S(1)} %shard_map.31.eps), channel_id=1, source_target_pairs={{0,16},{1,17},{2,18},{3,19},{4,20},{5,21},{6,22},{7,23},{8,24},{9,... | collective-permute-start | bytes 12296 | tf_op jit(solution)/shard_map/ppermute | solution.py:630
  3.9 2.1 %collective-permute-start.1 = (f32[8,128]{1,0:T(8,128)S(1)}, f32[8,128]{1,0:T(8,128)S(1)}, u32[]{:S(2)}, u32[]{:S(2)}) collective-permute-start(f32[8,128]{1,0:T(8,128)S(1)} %shard_map.31.eps), channel_id=1, source_target_pairs={{16,32},{17,33},{18,34},{19,35},{20,36},{21,37},{22,38},{23,39},{2... | collective-permute-start | bytes 12296 | tf_op jit(solution)/shard_map/ppermute | solution.py:630
  6.0 0.3 shard_map.32
  6.4 0.0 collective-permute-done.rkce
  6.4 2.1 %collective-permute-done.1.rkco = f32[8,128]{1,0:T(8,128)S(1)} collective-permute-done((f32[8,128]{1,0:T(8,128)S(1)}, f32[8,128]{1,0:T(8,128)S(1)}, u32[]{:S(2)}, u32[]{:S(2)}) %collective-permute-start.1) | collective-permute-done | bytes 4128 | tf_op jit(solution)/shard_map/ppermute | solution.py:630
  8.5 2.2 %collective-permute-start.3 = (f32[68,8,128]{2,1,0:T(8,128)S(1)}, f32[68,8,128]{2,1,0:T(8,128)S(1)}, u32[]{:S(2)}, u32[]{:S(2)}) collective-permute-start(f32[68,8,128]{2,1,0:T(8,128)S(1)} %get-tuple-element.22), channel_id=1, source_target_pairs={{0,1},{1,0},{2,3},{3,2},{4,5},{5,4},{6,7},{7,6},{8,9},{9,8},{10,11... | collective-permute-start | bytes 835592 | tf_op jit(solution)/shard_map/ppermute | solution.py:620
  10.7 2.0 %collective-permute-start.4 = (f32[65,8,128]{2,1,0:T(8,128)S(1)}, f32[65,8,128]{2,1,0:T(8,128)S(1)}, u32[]{:S(2)}, u32[]{:S(2)}) collective-permute-start(f32[65,8,128]{2,1,0:T(8,128)S(1)} %get-tuple-element.25), channel_id=1, source_target_pairs={{1,2},{2,1},{3,4},{4,3},{5,6},{6,5},{7,8},{8,7},{9,10},{10,9},{11,... | collective-permute-start | bytes 798728 | tf_op jit(solution)/shard_map/ppermute | solution.py:620
  12.7 0.3 shard_map.36
  13.0 0.1 collective-permute-start.5
  13.1 1.3 %collective-permute-start.2 = (f32[3,8,128]{2,1,0:T(8,128)S(1)}, f32[3,8,128]{2,1,0:T(8,128)S(1)}, u32[]{:S(2)}, u32[]{:S(2)}) collective-permute-start(f32[3,8,128]{2,1,0:T(8,128)S(1)} %get-tuple-element.21.three), channel_id=1, source_target_pairs={{1,2},{2,1},{3,4},{4,3},{5,6},{6,5},{7,8},{8,7},{9,10},{10,9},{11,... | collective-permute-start | bytes 36872 | tf_op jit(solution)/shard_map/ppermute | solution.py:620
  14.5 1.8 %shard_map.30 = (f32[5,125,8,128]{3,2,1,0:T(8,128)S(1)}, f32[5,125,8,128]{3,2,1,0:T(8,128)S(1)}) custom-call(f32[5,125,8,128]{3,2,1,0:T(8,128)S(1)} %bitcast.6), custom_call_target="tpu_custom_call" | custom-call | flops 16384000 | bytes 7680000 | tf_op jit(solution)/shard_map/pallas_call | solution.py:593
  16.3 4.9 %collective-permute-done.2.rkso = f32[3,8,128]{2,1,0:T(8,128)S(1)} collective-permute-done((f32[3,8,128]{2,1,0:T(8,128)S(1)}, f32[3,8,128]{2,1,0:T(8,128)S(1)}, u32[]{:S(2)}, u32[]{:S(2)}) %collective-permute-start.2) | collective-permute-done | bytes 12320 | tf_op jit(solution)/shard_map/ppermute | solution.py:620
  21.2 0.0 collective-permute-done.3.rse
  21.2 0.7 %shard_map.34 = (f32[125,8,128]{2,1,0:T(8,128)S(1)}, f32[36,8,128]{2,1,0:T(8,128)S(1)}, f32[36,8,128]{2,1,0:T(8,128)S(1)}, f32[4,8,128]{2,1,0:T(8,128)S(1)}) custom-call(f32[5,125,8,128]{3,2,1,0:T(8,128)S(1)} %get-tuple-element.19.gc, f32[3,8,128]{2,1,0:T(8,128)S(1)} %get-tuple-element.21.three, f32[3,8,128]{2,1,0:T(8,128)S(1)} %collective-permute-done.2.rkso, ...), custom_call_target="tpu_custom_call" | custom-call | flops 8192000 | bytes 3686400 | tf_op jit(solution)/shard_map/pallas_call | solution.py:593
  21.8 0.0 collective-permute-done.4.rso
  21.8 0.7 %shard_map.35 = (f32[5,125,8,128]{3,2,1,0:T(8,128)S(1)}, f32[65,8,128]{2,1,0:T(8,128)S(1)}, f32[65,8,128]{2,1,0:T(8,128)S(1)}) custom-call(f32[5,125,8,128]{3,2,1,0:T(8,128)S(1)} %get-tuple-element.24.gs, f32[125,8,128]{2,1,0:T(8,128)S(1)} %get-tuple-element.23.visc, f32[68,8,128]{2,1,0:T(8,128)S(1)} %collective-permute-done.3.rse, ...), custom_call_target="tpu_custom_call" | custom-call | flops 8192000 | bytes 6709248 | tf_op jit(solution)/shard_map/pallas_call | solution.py:593
  22.5 2.1 %collective-permute-start.10 = (f32[65,8,128]{2,1,0:T(8,128)S(1)}, f32[65,8,128]{2,1,0:T(8,128)S(1)}, u32[]{:S(2)}, u32[]{:S(2)}) collective-permute-start(f32[65,8,128]{2,1,0:T(8,128)S(1)} %get-tuple-element.34), channel_id=1, source_target_pairs={{1,2},{2,1},{3,4},{4,3},{5,6},{6,5},{7,8},{8,7},{9,10},{10,9},{11,... | collective-permute-start | bytes 798728 | tf_op jit(solution)/shard_map/ppermute | solution.py:620
  24.6 0.0 collective-permute-start.9
  24.6 0.0 collective-permute-start.7
  24.6 3.0 %collective-permute-start.8 = (f32[36,8,128]{2,1,0:T(8,128)S(1)}, f32[36,8,128]{2,1,0:T(8,128)S(1)}, u32[]{:S(2)}, u32[]{:S(2)}) collective-permute-start(f32[36,8,128]{2,1,0:T(8,128)S(1)} %get-tuple-element.31), channel_id=1, source_target_pairs={{16,32},{17,33},{18,34},{19,35},{20,36},{21,37},{22,38},{23,39},{2... | collective-permute-start | bytes 442376 | tf_op jit(solution)/shard_map/ppermute | solution.py:630
  27.6 0.0 collective-permute-done.5.rce
  27.7 0.5 %collective-permute-start.6 = (f32[35,8,128]{2,1,0:T(8,128)S(1)}, f32[35,8,128]{2,1,0:T(8,128)S(1)}, u32[]{:S(2)}, u32[]{:S(2)}) collective-permute-start(f32[35,8,128]{2,1,0:T(8,128)S(1)} %get-tuple-element.28.co), channel_id=1, source_target_pairs={{16,32},{17,33},{18,34},{19,35},{20,36},{21,37},{22,38},{23,39},{2... | collective-permute-start | bytes 430088 | tf_op jit(solution)/shard_map/ppermute | solution.py:630
  28.2 12.3 %collective-permute-done.6.rco = f32[35,8,128]{2,1,0:T(8,128)S(1)} collective-permute-done((f32[35,8,128]{2,1,0:T(8,128)S(1)}, f32[35,8,128]{2,1,0:T(8,128)S(1)}, u32[]{:S(2)}, u32[]{:S(2)}) %collective-permute-start.6) | collective-permute-done | bytes 143392 | tf_op jit(solution)/shard_map/ppermute | solution.py:630
  40.5 4.4 %shard_map.37 = (f32[5,125,8,128]{3,2,1,0:T(8,128)S(1)}, f32[125,8,128]{2,1,0:T(8,128)}) custom-call(f32[5,125,8,128]{3,2,1,0:T(8,128)S(1)} %bitcast.7, f32[125,8,128]{2,1,0:T(8,128)S(1)} %get-tuple-element.23.visc, f32[5,125,8,128]{3,2,1,0:T(8,128)S(1)} %get-tuple-element.26.fs, f32[5,125,8,128]{3,2,1,0:T(8,128)S(1)} %get-tuple-element.19.gc, ...), custom_call_target="tpu_custom_call" | custom-call | flops 32768000 | bytes 11550720 | tf_op jit(solution)/shard_map/pallas_call | solution.py:593
  44.9 0.0 collective-permute-done.7.rbce
  44.9 0.0 collective-permute-done.8.rbco
  44.9 0.4 shard_map.38.res
  45.3 0.0 collective-permute-done.10.rbso
  45.3 0.0 collective-permute-done.9.rbse
  45.3 1.7 %shard_map.39 = f32[5,125,8,128]{3,2,1,0:T(8,128)} custom-call(f32[5,125,8,128]{3,2,1,0:T(8,128)S(1)} %shard_map.38.res, f32[65,8,128]{2,1,0:T(8,128)S(1)} %collective-permute-done.9.rbse, f32[65,8,128]{2,1,0:T(8,128)S(1)} %collective-permute-done.10.rbso), custom_call_target="tpu_custom_call" | custom-call | flops 8192000 | bytes 5652480 | tf_op jit(solution)/shard_map/pallas_call | solution.py:593
  (2 shorter events, 0.0 us)
Async XLA Ops:
  0.6 5.4 %copy-start = (f32[5,125,4,2,128]{4,3,2,1,0:T(2,128)S(1)}, f32[5,125,4,2,128]{4,3,2,1,0:T(2,128)}, u32[]{:S(2)}) copy-start(f32[5,125,4,2,128]{4,3,2,1,0:T(2,128)} %param.1) | copy-start | bytes 7680004
  2.2 4.2 %collective-permute-start = (f32[8,128]{1,0:T(8,128)S(1)}, f32[8,128]{1,0:T(8,128)S(1)}, u32[]{:S(2)}, u32[]{:S(2)}) collective-permute-start(f32[8,128]{1,0:T(8,128)S(1)} %shard_map.31.eps), channel_id=1, source_target_pairs={{0,16},{1,17},{2,18},{3,19},{4,20},{5,21},{6,22},{7,23},{8,24},{9,... | collective-permute-start | bytes 12296 | tf_op jit(solution)/shard_map/ppermute | solution.py:630
  3.9 4.6 %collective-permute-start.1 = (f32[8,128]{1,0:T(8,128)S(1)}, f32[8,128]{1,0:T(8,128)S(1)}, u32[]{:S(2)}, u32[]{:S(2)}) collective-permute-start(f32[8,128]{1,0:T(8,128)S(1)} %shard_map.31.eps), channel_id=1, source_target_pairs={{16,32},{17,33},{18,34},{19,35},{20,36},{21,37},{22,38},{23,39},{2... | collective-permute-start | bytes 12296 | tf_op jit(solution)/shard_map/ppermute | solution.py:630
  8.5 12.6 %collective-permute-start.3 = (f32[68,8,128]{2,1,0:T(8,128)S(1)}, f32[68,8,128]{2,1,0:T(8,128)S(1)}, u32[]{:S(2)}, u32[]{:S(2)}) collective-permute-start(f32[68,8,128]{2,1,0:T(8,128)S(1)} %get-tuple-element.22), channel_id=1, source_target_pairs={{0,1},{1,0},{2,3},{3,2},{4,5},{5,4},{6,7},{7,6},{8,9},{9,8},{10,11... | collective-permute-start | bytes 835592 | tf_op jit(solution)/shard_map/ppermute | solution.py:620
  10.7 11.1 %collective-permute-start.4 = (f32[65,8,128]{2,1,0:T(8,128)S(1)}, f32[65,8,128]{2,1,0:T(8,128)S(1)}, u32[]{:S(2)}, u32[]{:S(2)}) collective-permute-start(f32[65,8,128]{2,1,0:T(8,128)S(1)} %get-tuple-element.25), channel_id=1, source_target_pairs={{1,2},{2,1},{3,4},{4,3},{5,6},{6,5},{7,8},{8,7},{9,10},{10,9},{11,... | collective-permute-start | bytes 798728 | tf_op jit(solution)/shard_map/ppermute | solution.py:620
  13.0 14.6 %collective-permute-start.5 = (f32[35,8,128]{2,1,0:T(8,128)S(1)}, f32[35,8,128]{2,1,0:T(8,128)S(1)}, u32[]{:S(2)}, u32[]{:S(2)}) collective-permute-start(f32[35,8,128]{2,1,0:T(8,128)S(1)} %get-tuple-element.27.ce), channel_id=1, source_target_pairs={{0,16},{1,17},{2,18},{3,19},{4,20},{5,21},{6,22},{7,23},{8,24},{9,... | collective-permute-start | bytes 430088 | tf_op jit(solution)/shard_map/ppermute | solution.py:630
  13.1 8.0 %collective-permute-start.2 = (f32[3,8,128]{2,1,0:T(8,128)S(1)}, f32[3,8,128]{2,1,0:T(8,128)S(1)}, u32[]{:S(2)}, u32[]{:S(2)}) collective-permute-start(f32[3,8,128]{2,1,0:T(8,128)S(1)} %get-tuple-element.21.three), channel_id=1, source_target_pairs={{1,2},{2,1},{3,4},{4,3},{5,6},{6,5},{7,8},{8,7},{9,10},{10,9},{11,... | collective-permute-start | bytes 36872 | tf_op jit(solution)/shard_map/ppermute | solution.py:620
  22.5 22.8 %collective-permute-start.10 = (f32[65,8,128]{2,1,0:T(8,128)S(1)}, f32[65,8,128]{2,1,0:T(8,128)S(1)}, u32[]{:S(2)}, u32[]{:S(2)}) collective-permute-start(f32[65,8,128]{2,1,0:T(8,128)S(1)} %get-tuple-element.34), channel_id=1, source_target_pairs={{1,2},{2,1},{3,4},{4,3},{5,6},{6,5},{7,8},{8,7},{9,10},{10,9},{11,... | collective-permute-start | bytes 798728 | tf_op jit(solution)/shard_map/ppermute | solution.py:620
  24.6 20.7 %collective-permute-start.9 = (f32[65,8,128]{2,1,0:T(8,128)S(1)}, f32[65,8,128]{2,1,0:T(8,128)S(1)}, u32[]{:S(2)}, u32[]{:S(2)}) collective-permute-start(f32[65,8,128]{2,1,0:T(8,128)S(1)} %get-tuple-element.33), channel_id=1, source_target_pairs={{0,1},{1,0},{2,3},{3,2},{4,5},{5,4},{6,7},{7,6},{8,9},{9,8},{10,11... | collective-permute-start | bytes 798728 | tf_op jit(solution)/shard_map/ppermute | solution.py:620
  24.6 20.3 %collective-permute-start.7 = (f32[36,8,128]{2,1,0:T(8,128)S(1)}, f32[36,8,128]{2,1,0:T(8,128)S(1)}, u32[]{:S(2)}, u32[]{:S(2)}) collective-permute-start(f32[36,8,128]{2,1,0:T(8,128)S(1)} %get-tuple-element.30), channel_id=1, source_target_pairs={{0,16},{1,17},{2,18},{3,19},{4,20},{5,21},{6,22},{7,23},{8,24},{9,... | collective-permute-start | bytes 442376 | tf_op jit(solution)/shard_map/ppermute | solution.py:630
  24.6 20.3 %collective-permute-start.8 = (f32[36,8,128]{2,1,0:T(8,128)S(1)}, f32[36,8,128]{2,1,0:T(8,128)S(1)}, u32[]{:S(2)}, u32[]{:S(2)}) collective-permute-start(f32[36,8,128]{2,1,0:T(8,128)S(1)} %get-tuple-element.31), channel_id=1, source_target_pairs={{16,32},{17,33},{18,34},{19,35},{20,36},{21,37},{22,38},{23,39},{2... | collective-permute-start | bytes 442376 | tf_op jit(solution)/shard_map/ppermute | solution.py:630
  27.7 12.9 %collective-permute-start.6 = (f32[35,8,128]{2,1,0:T(8,128)S(1)}, f32[35,8,128]{2,1,0:T(8,128)S(1)}, u32[]{:S(2)}, u32[]{:S(2)}) collective-permute-start(f32[35,8,128]{2,1,0:T(8,128)S(1)} %get-tuple-element.28.co), channel_id=1, source_target_pairs={{16,32},{17,33},{18,34},{19,35},{20,36},{21,37},{22,38},{23,39},{2... | collective-permute-start | bytes 430088 | tf_op jit(solution)/shard_map/ppermute | solution.py:630
where the time goes:
time: 47.2 us; the launch traced here: 47.1 us
  waiting for transfers between devices  19.3 us (41%)
  starting transfers between devices  15.1 us (32%)
  Pallas kernels  11.9 us (25%)
  between operations  0.76 us (2%)
    ppermute x6, waiting for transfers between devices, chord_swap(): return lax.ppermute(array, ('chord', 'span'), route)  14.4 us
    pallas_call x10, Pallas kernels, call(): pl.pallas_call(kernel, out_shape=outs, in_specs=[hbm if n in far_in else...  11.9 us
    ppermute x5, starting transfers between devices, span_swap(): return lax.ppermute(array, 'span', paired(spans, odd, True))  7.59 us
    ppermute x6, starting transfers between devices, chord_swap(): return lax.ppermute(array, ('chord', 'span'), route)  7.51 us
    ppermute x5, waiting for transfers between devices, span_swap(): return lax.ppermute(array, 'span', paired(spans, odd, True))  4.91 us
  transfers between devices with their start and end apart: 11, of which 3 were waited for; matrix products, arithmetic and copies ran while one was open for 0% of the time, Pallas kernels for 18%

commit v1 on v0

--- a/solution.py
+++ b/solution.py
@@ -530,40 +530,35 @@
     lax.fori_loop(0, NV, one, 0)
 
 
-def close_span_kernel(res, rbse, rbso, final, out, sems):
+def close_span_kernel(res, rbse, rbso, final, edge, out, sems):
     _, j = row_ids()
     is_low = j == 0
     es = even_span()
     weights = span_weights(is_low)
 
-    def send(v, a):
-        points = pl.ds(NF * a, NF)
-        return pltpu.make_async_copy(out.at[v, points], final.at[v, points], sems.at[v, a])
+    def send(v):
+        return pltpu.make_async_copy(out.at[v], final.at[v], sems.at[v])
 
     def one(v, carry):
         for m in range(SPAN_V):
             first, second = rbse[v * SPAN_V + m], rbso[v * SPAN_V + m]
             behind, ahead = jnp.where(es, second, first), jnp.where(es, first, second)
             for f in range(2 * m, min(2 * m + 2, NF)):
-                edge = open_span(behind, ahead, f % 2, is_low)
-                for k, p in enumerate(line_points(1, f)):
-                    out[v, p] = res[v, p] + weights[k] * edge
-                a, c = f // 5, f % 5
-                if c == 4 and a > 0:
-                    send(v, a - 1).start()
-                elif c == 4:
-
-                    @pl.when(v > 0)
-                    def _():
-                        send(v - 1, 4).start()
-
-        return carry
-
-    lax.fori_loop(0, NV, one, 0)
-    send(NV - 1, 4).start()
+                edge[f] = open_span(behind, ahead, f % 2, is_low)
+        for f in range(NF):
+            for k, p in enumerate(line_points(1, f)):
+                out[v, p] = res[v, p] + weights[k] * edge[f]
+
+        @pl.when(v > 0)
+        def _():
+            send(v - 1).start()
+
+        return carry
+
+    lax.fori_loop(0, NV, one, 0)
+    send(NV - 1).start()
     for v in range(NV):
-        for a in range(5):
-            send(v, a).wait()
+        send(v).wait()
 
 
 def span_weights(is_low):
@@ -680,7 +675,7 @@
         close_span_kernel,
         [vec(NV, 125)],
         [res, rbse, rbso],
-        [held(NV, 125), dma((NV, 5))],
+        [held(NF), held(NV, 125), dma((NV,))],
         cycles=2000,
         far_out=(0,),
     )

time: 47.2 us -> 47.1 us (level)
  no operation moved by 1% of the time
where the time goes in v1:
time: 47.1 us; the launch traced here: 47 us
  waiting for transfers between devices  19.3 us (41%)
  starting transfers between devices  15.1 us (32%)
  Pallas kernels  11.8 us (25%)
  between operations  0.76 us (2%)
    ppermute x6, waiting for transfers between devices, chord_swap(): return lax.ppermute(array, ('chord', 'span'), route)  14.4 us
    pallas_call x10, Pallas kernels, call(): pl.pallas_call(kernel, out_shape=outs, in_specs=[hbm if n in far_in else...  11.8 us
    ppermute x5, starting transfers between devices, span_swap(): return lax.ppermute(array, 'span', paired(spans, odd, True))  7.59 us
    ppermute x6, starting transfers between devices, chord_swap(): return lax.ppermute(array, ('chord', 'span'), route)  7.51 us
    ppermute x5, waiting for transfers between devices, span_swap(): return lax.ppermute(array, 'span', paired(spans, odd, True))  4.91 us
  transfers between devices with their start and end apart: 11, of which 3 were waited for; matrix products, arithmetic and copies ran while one was open for 0% of the time, Pallas kernels for 18%

profile of v1, /device:TPU:15, one launch (start us, length us, event | category | flops | bytes accessed | tf_op | source)
XLA Modules:
  0.0 47.0 jit_solution(7543754938375180046)
XLA Ops:
  0.6 0.0 copy-start
  0.6 1.6 %shard_map.31.eps = f32[8,128]{1,0:T(8,128)S(1)} custom-call(f32[5,125,8,128]{3,2,1,0:T(8,128)} %bitcast.3), custom_call_target="tpu_custom_call" | custom-call | flops 4096000 | bytes 2564096 | tf_op jit(solution)/shard_map/pallas_call | solution.py:588
  2.2 1.7 %collective-permute-start = (f32[8,128]{1,0:T(8,128)S(1)}, f32[8,128]{1,0:T(8,128)S(1)}, u32[]{:S(2)}, u32[]{:S(2)}) collective-permute-start(f32[8,128]{1,0:T(8,128)S(1)} %shard_map.31.eps), channel_id=1, source_target_pairs={{0,16},{1,17},{2,18},{3,19},{4,20},{5,21},{6,22},{7,23},{8,24},{9,... | collective-permute-start | bytes 12296 | tf_op jit(solution)/shard_map/ppermute | solution.py:625
  3.9 2.1 %collective-permute-start.1 = (f32[8,128]{1,0:T(8,128)S(1)}, f32[8,128]{1,0:T(8,128)S(1)}, u32[]{:S(2)}, u32[]{:S(2)}) collective-permute-start(f32[8,128]{1,0:T(8,128)S(1)} %shard_map.31.eps), channel_id=1, source_target_pairs={{16,32},{17,33},{18,34},{19,35},{20,36},{21,37},{22,38},{23,39},{2... | collective-permute-start | bytes 12296 | tf_op jit(solution)/shard_map/ppermute | solution.py:625
  6.0 0.3 shard_map.32
  6.4 0.0 collective-permute-done.rkce
  6.4 2.1 %collective-permute-done.1.rkco = f32[8,128]{1,0:T(8,128)S(1)} collective-permute-done((f32[8,128]{1,0:T(8,128)S(1)}, f32[8,128]{1,0:T(8,128)S(1)}, u32[]{:S(2)}, u32[]{:S(2)}) %collective-permute-start.1) | collective-permute-done | bytes 4128 | tf_op jit(solution)/shard_map/ppermute | solution.py:625
  8.5 2.2 %collective-permute-start.3 = (f32[68,8,128]{2,1,0:T(8,128)S(1)}, f32[68,8,128]{2,1,0:T(8,128)S(1)}, u32[]{:S(2)}, u32[]{:S(2)}) collective-permute-start(f32[68,8,128]{2,1,0:T(8,128)S(1)} %get-tuple-element.22), channel_id=1, source_target_pairs={{0,1},{1,0},{2,3},{3,2},{4,5},{5,4},{6,7},{7,6},{8,9},{9,8},{10,11... | collective-permute-start | bytes 835592 | tf_op jit(solution)/shard_map/ppermute | solution.py:615
  10.7 2.0 %collective-permute-start.4 = (f32[65,8,128]{2,1,0:T(8,128)S(1)}, f32[65,8,128]{2,1,0:T(8,128)S(1)}, u32[]{:S(2)}, u32[]{:S(2)}) collective-permute-start(f32[65,8,128]{2,1,0:T(8,128)S(1)} %get-tuple-element.25), channel_id=1, source_target_pairs={{1,2},{2,1},{3,4},{4,3},{5,6},{6,5},{7,8},{8,7},{9,10},{10,9},{11,... | collective-permute-start | bytes 798728 | tf_op jit(solution)/shard_map/ppermute | solution.py:615
  12.7 0.3 shard_map.36
  13.0 0.1 collective-permute-start.5
  13.1 1.3 %collective-permute-start.2 = (f32[3,8,128]{2,1,0:T(8,128)S(1)}, f32[3,8,128]{2,1,0:T(8,128)S(1)}, u32[]{:S(2)}, u32[]{:S(2)}) collective-permute-start(f32[3,8,128]{2,1,0:T(8,128)S(1)} %get-tuple-element.21.three), channel_id=1, source_target_pairs={{1,2},{2,1},{3,4},{4,3},{5,6},{6,5},{7,8},{8,7},{9,10},{10,9},{11,... | collective-permute-start | bytes 36872 | tf_op jit(solution)/shard_map/ppermute | solution.py:615
  14.5 1.8 %shard_map.30 = (f32[5,125,8,128]{3,2,1,0:T(8,128)S(1)}, f32[5,125,8,128]{3,2,1,0:T(8,128)S(1)}) custom-call(f32[5,125,8,128]{3,2,1,0:T(8,128)S(1)} %bitcast.6), custom_call_target="tpu_custom_call" | custom-call | flops 16384000 | bytes 7680000 | tf_op jit(solution)/shard_map/pallas_call | solution.py:588
  16.3 4.9 %collective-permute-done.2.rkso = f32[3,8,128]{2,1,0:T(8,128)S(1)} collective-permute-done((f32[3,8,128]{2,1,0:T(8,128)S(1)}, f32[3,8,128]{2,1,0:T(8,128)S(1)}, u32[]{:S(2)}, u32[]{:S(2)}) %collective-permute-start.2) | collective-permute-done | bytes 12320 | tf_op jit(solution)/shard_map/ppermute | solution.py:615
  21.2 0.0 collective-permute-done.3.rse
  21.2 0.7 %shard_map.34 = (f32[125,8,128]{2,1,0:T(8,128)S(1)}, f32[36,8,128]{2,1,0:T(8,128)S(1)}, f32[36,8,128]{2,1,0:T(8,128)S(1)}, f32[4,8,128]{2,1,0:T(8,128)S(1)}) custom-call(f32[5,125,8,128]{3,2,1,0:T(8,128)S(1)} %get-tuple-element.19.gc, f32[3,8,128]{2,1,0:T(8,128)S(1)} %get-tuple-element.21.three, f32[3,8,128]{2,1,0:T(8,128)S(1)} %collective-permute-done.2.rkso, ...), custom_call_target="tpu_custom_call" | custom-call | flops 8192000 | bytes 3686400 | tf_op jit(solution)/shard_map/pallas_call | solution.py:588
  21.8 0.0 collective-permute-done.4.rso
  21.8 0.7 %shard_map.35 = (f32[5,125,8,128]{3,2,1,0:T(8,128)S(1)}, f32[65,8,128]{2,1,0:T(8,128)S(1)}, f32[65,8,128]{2,1,0:T(8,128)S(1)}) custom-call(f32[5,125,8,128]{3,2,1,0:T(8,128)S(1)} %get-tuple-element.24.gs, f32[125,8,128]{2,1,0:T(8,128)S(1)} %get-tuple-element.23.visc, f32[68,8,128]{2,1,0:T(8,128)S(1)} %collective-permute-done.3.rse, ...), custom_call_target="tpu_custom_call" | custom-call | flops 8192000 | bytes 6709248 | tf_op jit(solution)/shard_map/pallas_call | solution.py:588
  22.5 2.1 %collective-permute-start.10 = (f32[65,8,128]{2,1,0:T(8,128)S(1)}, f32[65,8,128]{2,1,0:T(8,128)S(1)}, u32[]{:S(2)}, u32[]{:S(2)}) collective-permute-start(f32[65,8,128]{2,1,0:T(8,128)S(1)} %get-tuple-element.34), channel_id=1, source_target_pairs={{1,2},{2,1},{3,4},{4,3},{5,6},{6,5},{7,8},{8,7},{9,10},{10,9},{11,... | collective-permute-start | bytes 798728 | tf_op jit(solution)/shard_map/ppermute | solution.py:615
  24.6 0.0 collective-permute-start.9
  24.6 0.0 collective-permute-start.7
  24.6 3.0 %collective-permute-start.8 = (f32[36,8,128]{2,1,0:T(8,128)S(1)}, f32[36,8,128]{2,1,0:T(8,128)S(1)}, u32[]{:S(2)}, u32[]{:S(2)}) collective-permute-start(f32[36,8,128]{2,1,0:T(8,128)S(1)} %get-tuple-element.31), channel_id=1, source_target_pairs={{16,32},{17,33},{18,34},{19,35},{20,36},{21,37},{22,38},{23,39},{2... | collective-permute-start | bytes 442376 | tf_op jit(solution)/shard_map/ppermute | solution.py:625
  27.6 0.0 collective-permute-done.5.rce
  27.7 0.5 %collective-permute-start.6 = (f32[35,8,128]{2,1,0:T(8,128)S(1)}, f32[35,8,128]{2,1,0:T(8,128)S(1)}, u32[]{:S(2)}, u32[]{:S(2)}) collective-permute-start(f32[35,8,128]{2,1,0:T(8,128)S(1)} %get-tuple-element.28.co), channel_id=1, source_target_pairs={{16,32},{17,33},{18,34},{19,35},{20,36},{21,37},{22,38},{23,39},{2... | collective-permute-start | bytes 430088 | tf_op jit(solution)/shard_map/ppermute | solution.py:625
  28.2 12.3 %collective-permute-done.6.rco = f32[35,8,128]{2,1,0:T(8,128)S(1)} collective-permute-done((f32[35,8,128]{2,1,0:T(8,128)S(1)}, f32[35,8,128]{2,1,0:T(8,128)S(1)}, u32[]{:S(2)}, u32[]{:S(2)}) %collective-permute-start.6) | collective-permute-done | bytes 143392 | tf_op jit(solution)/shard_map/ppermute | solution.py:625
  40.5 4.4 %shard_map.37 = (f32[5,125,8,128]{3,2,1,0:T(8,128)S(1)}, f32[125,8,128]{2,1,0:T(8,128)}) custom-call(f32[5,125,8,128]{3,2,1,0:T(8,128)S(1)} %bitcast.7, f32[125,8,128]{2,1,0:T(8,128)S(1)} %get-tuple-element.23.visc, f32[5,125,8,128]{3,2,1,0:T(8,128)S(1)} %get-tuple-element.26.fs, f32[5,125,8,128]{3,2,1,0:T(8,128)S(1)} %get-tuple-element.19.gc, ...), custom_call_target="tpu_custom_call" | custom-call | flops 32768000 | bytes 11550720 | tf_op jit(solution)/shard_map/pallas_call | solution.py:588
  44.9 0.0 collective-permute-done.7.rbce
  44.9 0.0 collective-permute-done.8.rbco
  44.9 0.4 shard_map.38.res
  45.3 0.0 collective-permute-done.10.rbso
  45.3 0.0 collective-permute-done.9.rbse
  45.3 1.6 %shard_map.39 = f32[5,125,8,128]{3,2,1,0:T(8,128)} custom-call(f32[5,125,8,128]{3,2,1,0:T(8,128)S(1)} %shard_map.38.res, f32[65,8,128]{2,1,0:T(8,128)S(1)} %collective-permute-done.9.rbse, f32[65,8,128]{2,1,0:T(8,128)S(1)} %collective-permute-done.10.rbso), custom_call_target="tpu_custom_call" | custom-call | flops 8192000 | bytes 5652480 | tf_op jit(solution)/shard_map/pallas_call | solution.py:588
  (2 shorter events, 0.0 us)
Async XLA Ops:
  0.6 5.4 %copy-start = (f32[5,125,4,2,128]{4,3,2,1,0:T(2,128)S(1)}, f32[5,125,4,2,128]{4,3,2,1,0:T(2,128)}, u32[]{:S(2)}) copy-start(f32[5,125,4,2,128]{4,3,2,1,0:T(2,128)} %param.1) | copy-start | bytes 7680004
  2.2 4.2 %collective-permute-start = (f32[8,128]{1,0:T(8,128)S(1)}, f32[8,128]{1,0:T(8,128)S(1)}, u32[]{:S(2)}, u32[]{:S(2)}) collective-permute-start(f32[8,128]{1,0:T(8,128)S(1)} %shard_map.31.eps), channel_id=1, source_target_pairs={{0,16},{1,17},{2,18},{3,19},{4,20},{5,21},{6,22},{7,23},{8,24},{9,... | collective-permute-start | bytes 12296 | tf_op jit(solution)/shard_map/ppermute | solution.py:625
  3.9 4.6 %collective-permute-start.1 = (f32[8,128]{1,0:T(8,128)S(1)}, f32[8,128]{1,0:T(8,128)S(1)}, u32[]{:S(2)}, u32[]{:S(2)}) collective-permute-start(f32[8,128]{1,0:T(8,128)S(1)} %shard_map.31.eps), channel_id=1, source_target_pairs={{16,32},{17,33},{18,34},{19,35},{20,36},{21,37},{22,38},{23,39},{2... | collective-permute-start | bytes 12296 | tf_op jit(solution)/shard_map/ppermute | solution.py:625
  8.5 12.6 %collective-permute-start.3 = (f32[68,8,128]{2,1,0:T(8,128)S(1)}, f32[68,8,128]{2,1,0:T(8,128)S(1)}, u32[]{:S(2)}, u32[]{:S(2)}) collective-permute-start(f32[68,8,128]{2,1,0:T(8,128)S(1)} %get-tuple-element.22), channel_id=1, source_target_pairs={{0,1},{1,0},{2,3},{3,2},{4,5},{5,4},{6,7},{7,6},{8,9},{9,8},{10,11... | collective-permute-start | bytes 835592 | tf_op jit(solution)/shard_map/ppermute | solution.py:615
  10.7 11.1 %collective-permute-start.4 = (f32[65,8,128]{2,1,0:T(8,128)S(1)}, f32[65,8,128]{2,1,0:T(8,128)S(1)}, u32[]{:S(2)}, u32[]{:S(2)}) collective-permute-start(f32[65,8,128]{2,1,0:T(8,128)S(1)} %get-tuple-element.25), channel_id=1, source_target_pairs={{1,2},{2,1},{3,4},{4,3},{5,6},{6,5},{7,8},{8,7},{9,10},{10,9},{11,... | collective-permute-start | bytes 798728 | tf_op jit(solution)/shard_map/ppermute | solution.py:615
  13.0 14.6 %collective-permute-start.5 = (f32[35,8,128]{2,1,0:T(8,128)S(1)}, f32[35,8,128]{2,1,0:T(8,128)S(1)}, u32[]{:S(2)}, u32[]{:S(2)}) collective-permute-start(f32[35,8,128]{2,1,0:T(8,128)S(1)} %get-tuple-element.27.ce), channel_id=1, source_target_pairs={{0,16},{1,17},{2,18},{3,19},{4,20},{5,21},{6,22},{7,23},{8,24},{9,... | collective-permute-start | bytes 430088 | tf_op jit(solution)/shard_map/ppermute | solution.py:625
  13.1 8.0 %collective-permute-start.2 = (f32[3,8,128]{2,1,0:T(8,128)S(1)}, f32[3,8,128]{2,1,0:T(8,128)S(1)}, u32[]{:S(2)}, u32[]{:S(2)}) collective-permute-start(f32[3,8,128]{2,1,0:T(8,128)S(1)} %get-tuple-element.21.three), channel_id=1, source_target_pairs={{1,2},{2,1},{3,4},{4,3},{5,6},{6,5},{7,8},{8,7},{9,10},{10,9},{11,... | collective-permute-start | bytes 36872 | tf_op jit(solution)/shard_map/ppermute | solution.py:615
  22.5 22.8 %collective-permute-start.10 = (f32[65,8,128]{2,1,0:T(8,128)S(1)}, f32[65,8,128]{2,1,0:T(8,128)S(1)}, u32[]{:S(2)}, u32[]{:S(2)}) collective-permute-start(f32[65,8,128]{2,1,0:T(8,128)S(1)} %get-tuple-element.34), channel_id=1, source_target_pairs={{1,2},{2,1},{3,4},{4,3},{5,6},{6,5},{7,8},{8,7},{9,10},{10,9},{11,... | collective-permute-start | bytes 798728 | tf_op jit(solution)/shard_map/ppermute | solution.py:615
  24.6 20.7 %collective-permute-start.9 = (f32[65,8,128]{2,1,0:T(8,128)S(1)}, f32[65,8,128]{2,1,0:T(8,128)S(1)}, u32[]{:S(2)}, u32[]{:S(2)}) collective-permute-start(f32[65,8,128]{2,1,0:T(8,128)S(1)} %get-tuple-element.33), channel_id=1, source_target_pairs={{0,1},{1,0},{2,3},{3,2},{4,5},{5,4},{6,7},{7,6},{8,9},{9,8},{10,11... | collective-permute-start | bytes 798728 | tf_op jit(solution)/shard_map/ppermute | solution.py:615
  24.6 20.3 %collective-permute-start.7 = (f32[36,8,128]{2,1,0:T(8,128)S(1)}, f32[36,8,128]{2,1,0:T(8,128)S(1)}, u32[]{:S(2)}, u32[]{:S(2)}) collective-permute-start(f32[36,8,128]{2,1,0:T(8,128)S(1)} %get-tuple-element.30), channel_id=1, source_target_pairs={{0,16},{1,17},{2,18},{3,19},{4,20},{5,21},{6,22},{7,23},{8,24},{9,... | collective-permute-start | bytes 442376 | tf_op jit(solution)/shard_map/ppermute | solution.py:625
  24.6 20.3 %collective-permute-start.8 = (f32[36,8,128]{2,1,0:T(8,128)S(1)}, f32[36,8,128]{2,1,0:T(8,128)S(1)}, u32[]{:S(2)}, u32[]{:S(2)}) collective-permute-start(f32[36,8,128]{2,1,0:T(8,128)S(1)} %get-tuple-element.31), channel_id=1, source_target_pairs={{16,32},{17,33},{18,34},{19,35},{20,36},{21,37},{22,38},{23,39},{2... | collective-permute-start | bytes 442376 | tf_op jit(solution)/shard_map/ppermute | solution.py:625
  27.7 12.9 %collective-permute-start.6 = (f32[35,8,128]{2,1,0:T(8,128)S(1)}, f32[35,8,128]{2,1,0:T(8,128)S(1)}, u32[]{:S(2)}, u32[]{:S(2)}) collective-permute-start(f32[35,8,128]{2,1,0:T(8,128)S(1)} %get-tuple-element.28.co), channel_id=1, source_target_pairs={{16,32},{17,33},{18,34},{19,35},{20,36},{21,37},{22,38},{23,39},{2... | collective-permute-start | bytes 430088 | tf_op jit(solution)/shard_map/ppermute | solution.py:625
